TPU v7x, 8 devices: a whole 2x2x1 slice. The times are simulated.
8 devices in a mesh: row: 2 (over z, y), col: 4 (over x, core).
Axes of the slice: x: 2, y: 2, z: 1, core: 2. Of those that a mesh axis runs over, the one named last changes fastest.
Arguments:
- v_mat: float32 [4096, 4096], P('row', 'col')
- t_fac: float32 [128, 32, 32], P('col')
- z_vec: float32 [4096, 1024], P(None, ('col', 'row'))
Outputs:
- output: float32 [4096, 1024], P('row', 'col')
All inputs are finite; a program needn't handle non-finite values.
Results may differ from a plain program's by a relative error of at most 0.001.
Values sent between devices are 32-bit elements.
A program may use at most 1 GiB of HBM per device.

v0:
```python
import jax
import jax.numpy as jnp
from jax import lax
from jax.sharding import PartitionSpec as P

FULL_PREC = lax.Precision.HIGHEST


def solution(mesh):
    col_shards = mesh.shape['col']

    def local_body(v_loc, t_loc, z_loc):
        panel_width = t_loc.shape[1]
        local_panels = t_loc.shape[0]
        num_panels = local_panels * col_shards
        my_col = lax.axis_index('col')
        t_all = lax.all_gather(t_loc, 'col', axis=0, tiled=True)
        x_loc = lax.all_to_all(z_loc, 'row', 0, 1, tiled=True)

        def panel_step(step_idx, x_cur):
            panel_idx = num_panels - 1 - step_idx
            owner_col = panel_idx % col_shards
            loc_slot = panel_idx // col_shards
            v_blk = lax.dynamic_slice_in_dim(v_loc, loc_slot * panel_width, panel_width, axis=1)
            v_pan = lax.psum(jnp.where(my_col == owner_col, v_blk, 0.0), 'col')
            t_pan = lax.dynamic_index_in_dim(t_all, owner_col * local_panels + loc_slot, axis=0, keepdims=False)
            w_part = jnp.einsum('nb,nk->bk', v_pan, x_cur, preferred_element_type=jnp.float32, precision=FULL_PREC)
            w_full = lax.psum(w_part, 'row')
            y_blk = jnp.dot(t_pan, w_full, preferred_element_type=jnp.float32, precision=FULL_PREC)
            return x_cur - jnp.dot(v_pan, y_blk, preferred_element_type=jnp.float32, precision=FULL_PREC)

        return lax.fori_loop(0, num_panels, panel_step, x_loc)

    return jax.shard_map(local_body, mesh=mesh,
                         in_specs=(P('row', 'col'), P('col', None, None), P(None, ('col', 'row'))),
                         out_specs=P('row', 'col'), check_vma=False)
```

profile of v0, /device:TPU:0, one launch (start us, length us, event | category | flops | bytes accessed | tf_op | source)
XLA Modules:
  0.0 6244.5 jit_solution(12367812814210537186)
XLA Ops:
  40.7 6195.6 %while.15 = (s32[]{:T(128)}, f32[2048,256]{1,0:T(8,128)S(1)}, s32[]{:T(128)}, f32[2048,1024]{1,0:T(8,128)}, f32[128,32,32]{2,1,0:T(8,128)}, /*index=5*/s32[]{:T(...) while((s32[]{:T(128)}, f32[2048,256]{1,0:T(8,128)S(1)}, ...), condition=%wide.region_3.4_spmd, body=%wide.region_0.3_spmd.sunk | while | flops 406462496 | bytes 11747858 | solution.py:32
  43.4 31.6 all-reduce.2.cloned.1.call-done
  92.7 30.8 all-reduce.2.cloned.1.call-done
  334.5 30.8 all-reduce.2.cloned.1.call-done
  383.0 30.8 all-reduce.2.cloned.1.call-done
  625.2 30.8 all-reduce.2.cloned.1.call-done
  914.9 30.8 all-reduce.2.cloned.1.call-done
  1060.3 30.8 all-reduce.2.cloned.1.call-done
  1205.6 30.8 all-reduce.2.cloned.1.call-done
  1689.9 30.8 all-reduce.2.cloned.1.call-done
  1834.9 30.8 all-reduce.2.cloned.1.call-done
  1980.2 30.8 all-reduce.2.cloned.1.call-done
  2125.5 30.8 all-reduce.2.cloned.1.call-done
  2415.3 30.8 all-reduce.2.cloned.1.call-done
  2657.4 30.8 all-reduce.2.cloned.1.call-done
  2705.9 30.8 all-reduce.2.cloned.1.call-done
  2948.0 30.8 all-reduce.2.cloned.1.call-done
  3141.6 30.8 all-reduce.2.cloned.1.call-done
  3286.6 30.8 all-reduce.2.cloned.1.call-done
  3625.2 30.8 all-reduce.2.cloned.1.call-done
  3770.5 30.8 all-reduce.2.cloned.1.call-done
  3867.6 30.8 all-reduce.2.cloned.1.call-done
  4109.8 30.8 all-reduce.2.cloned.1.call-done
  4351.6 30.8 all-reduce.2.cloned.1.call-done
  4593.7 30.8 all-reduce.2.cloned.1.call-done
  4883.7 30.8 all-reduce.2.cloned.1.call-done
  5125.5 30.8 all-reduce.2.cloned.1.call-done
  5367.6 30.8 all-reduce.2.cloned.1.call-done
  5464.7 30.8 all-reduce.2.cloned.1.call-done
  5610.1 30.8 all-reduce.2.cloned.1.call-done
  5948.7 30.8 all-reduce.2.cloned.1.call-done
  6190.5 30.8 all-reduce.2.cloned.1.call-done
  (1258 shorter events, 5260.1 us)
Async XLA Ops:
  40.7 34.3 all-reduce.2.cloned.1.call-start
  90.0 33.5 all-reduce.2.cloned.1.call-start
  331.8 33.5 all-reduce.2.cloned.1.call-start
  380.4 33.5 all-reduce.2.cloned.1.call-start
  622.5 33.5 all-reduce.2.cloned.1.call-start
  912.3 33.5 all-reduce.2.cloned.1.call-start
  1057.6 33.5 all-reduce.2.cloned.1.call-start
  1202.9 33.5 all-reduce.2.cloned.1.call-start
  1687.2 33.5 all-reduce.2.cloned.1.call-start
  1832.2 33.5 all-reduce.2.cloned.1.call-start
  1977.5 33.5 all-reduce.2.cloned.1.call-start
  2122.9 33.5 all-reduce.2.cloned.1.call-start
  2412.6 33.5 all-reduce.2.cloned.1.call-start
  2654.7 33.5 all-reduce.2.cloned.1.call-start
  2703.3 33.5 all-reduce.2.cloned.1.call-start
  2945.4 33.5 all-reduce.2.cloned.1.call-start
  3138.9 33.5 all-reduce.2.cloned.1.call-start
  3283.9 33.5 all-reduce.2.cloned.1.call-start
  3622.5 33.5 all-reduce.2.cloned.1.call-start
  3767.9 33.5 all-reduce.2.cloned.1.call-start
  3865.0 33.5 all-reduce.2.cloned.1.call-start
  4107.1 33.5 all-reduce.2.cloned.1.call-start
  4348.9 33.5 all-reduce.2.cloned.1.call-start
  4591.1 33.5 all-reduce.2.cloned.1.call-start
  4639.6 33.5 all-reduce.2.cloned.1.call-start
  4881.1 33.5 all-reduce.2.cloned.1.call-start
  5122.9 33.5 all-reduce.2.cloned.1.call-start
  5365.0 33.5 all-reduce.2.cloned.1.call-start
  5462.1 33.5 all-reduce.2.cloned.1.call-start
  5607.4 33.5 all-reduce.2.cloned.1.call-start
  5946.0 33.5 all-reduce.2.cloned.1.call-start
  6187.8 33.5 all-reduce.2.cloned.1.call-start
  (227 other events, 4814.8 us)
Sparse Core Ops, SparseCore 0:
  43.9 31.0 all-reduce.1
  93.2 30.2 all-reduce.1
  141.7 30.2 all-reduce.1
  383.5 30.2 all-reduce.1
  432.1 30.2 all-reduce.1
  722.2 30.2 all-reduce.1
  818.6 30.2 all-reduce.1
  915.4 30.2 all-reduce.1
  1302.6 30.2 all-reduce.1
  1399.7 30.2 all-reduce.1
  1932.1 30.2 all-reduce.1
  2126.0 30.2 all-reduce.1
  2222.5 30.2 all-reduce.1
  2512.5 30.2 all-reduce.1
  2609.3 30.2 all-reduce.1
  2900.0 30.2 all-reduce.1
  3142.1 30.2 all-reduce.1
  3238.6 30.2 all-reduce.1
  3287.1 30.2 all-reduce.1
  3335.7 30.2 all-reduce.1
  3432.4 30.2 all-reduce.1
  3673.9 30.2 all-reduce.1
  3722.5 30.2 all-reduce.1
  3819.6 30.2 all-reduce.1
  4013.5 30.2 all-reduce.1
  4303.5 30.2 all-reduce.1
  4400.7 30.2 all-reduce.1
  4835.7 30.2 all-reduce.1
  4884.2 30.2 all-reduce.1
  4932.8 30.2 all-reduce.1
  5222.8 30.2 all-reduce.1
  5900.6 30.2 all-reduce.1
  (96 shorter events, 2900.4 us)
where the time goes:
time: 6260 us; the launch traced here: 6240 us
  waiting for transfers between devices  3930 us (63%)
  blocking collectives  1090 us (17%)
  matrix products  859 us (14%)
  other arithmetic  325 us (5%)
    psum x128, waiting for transfers between devices, panel_step(): v_pan = lax.psum(jnp.where(my_col == owner_col, v_blk, 0.0), 'col')  3930 us
    psum x128, blocking collectives, panel_step(): w_full = lax.psum(w_part, 'row')  1060 us
    dot_general x128, matrix products, panel_step(): jnp.einsum('nb,nk->bk', v_pan, x_cur, preferred_element_type=jnp.float32,...  405 us
    dot_general x128, matrix products, panel_step(): jnp.dot(v_pan, y_blk, preferred_element_type=jnp.float32, precision=FULL_...  341 us
    select_n x128, other arithmetic, panel_step(): v_pan = lax.psum(jnp.where(my_col == owner_col, v_blk, 0.0), 'col')  325 us
  transfers between devices with their start and end apart: 129, of which 129 were waited for; matrix products, arithmetic and copies ran while one was open for 0% of the time, Pallas kernels for 0%

commit v1 on v0

v1 whole, which is shorter than its diff:
```python
import functools

import jax
import jax.numpy as jnp
from jax import lax
from jax.experimental import pallas as pl
from jax.experimental.pallas import tpu as pltpu
from jax.sharding import PartitionSpec as P

MESH = pl.DeviceIdType.MESH
F32, BF16 = jnp.float32, jnp.bfloat16
STEPS = 16
OFF = [k * (k - 1) // 2 for k in range(STEPS + 2)]
NT = (((1,), (1,)), ((), ()))
NN = (((1,), (0,)), ((), ()))
FX, FY, DX, DY, SO, SX, SY, SD, SE, LO = range(10)
TX, TY, TS, GX, GY, HX, HY, HD, HE = range(9)


def split3(a):
    p1 = a.astype(BF16)
    rest = a - p1.astype(F32)
    p2 = rest.astype(BF16)
    p3 = (rest - p2.astype(F32)).astype(BF16)
    return p1, p2, p3


def mul6(a, b, dims):
    dot = functools.partial(lax.dot_general, dimension_numbers=dims, preferred_element_type=F32)
    return (
        dot(a[0], b[0]) + dot(a[1], b[0]) + dot(a[2], b[0]) + dot(a[0], b[1]) + dot(a[1], b[1]) + dot(a[0], b[2])
    )


def mulf(a, b, dims=NN):
    return mul6(split3(a), split3(b), dims)


def kernel(vt_ref, tp_ref, z_ref, out_ref, land, tl, xt, vp, acc, yp, rs, ss, ts, zs, os):
    r, c = lax.axis_index("row"), lax.axis_index("col")
    cs = c + 1 - 2 * lax.rem(c, 2)
    cx = lax.rem(c + 2, 4)
    csx = lax.rem(cs + 2, 4)
    ry = 1 - r
    to_x, to_y, to_s = (r, cx), (ry, c), (r, cs)

    barrier = pltpu.get_barrier_semaphore()
    for dev in (to_x, to_y, to_s):
        pl.semaphore_signal(barrier, inc=1, device_id=dev, device_id_type=MESH)
    pl.semaphore_wait(barrier, 3)

    def seg(k, rr, cc, lo=0, n=None):
        return land.at[pl.ds(OFF[k] + lo, k if n is None else n), rr, :, cc]

    def remote(src, dst, send, recv, dev):
        return pltpu.make_async_remote_copy(
            src_ref=src, dst_ref=dst, send_sem=send, recv_sem=recv, device_id=dev, device_id_type=MESH
        )

    def own(k):
        return vt_ref.at[pl.ds(STEPS - k, k), pl.ds(2 * (STEPS - k), 2)]

    def halves(k):
        h = (k + 1) // 2 if k % 2 else k // 2
        if k % 4 == 1:
            h = k // 2
        return (0, h), (h, k - h)

    def c_own(k):
        return [
            remote(own(k), seg(k, r, c), ss.at[TX, k], rs.at[FX, k], to_x),
            remote(own(k), seg(k, r, c), ss.at[TY, k], rs.at[FY, k], to_y),
            remote(own(k), seg(k, r, c), ss.at[TS, k], rs.at[SO, k], to_s),
        ]

    def c_loc(k):
        return pltpu.make_async_copy(own(k), seg(k, r, c), rs.at[LO, k])

    def c_fwd(k):
        (a0, an), (b0, bn) = halves(k)
        out = []
        if an:
            out.append(remote(seg(k, r, cx, a0, an), seg(k, r, cx, a0, an), ss.at[GY, k], rs.at[DY, k], to_y))
        if bn:
            out.append(remote(seg(k, ry, c, b0, bn), seg(k, ry, c, b0, bn), ss.at[GX, k], rs.at[DX, k], to_x))
        return out

    def c_sib(k):
        return [
            remote(seg(k, r, cx), seg(k, r, cx), ss.at[HX, k], rs.at[SX, k], to_s),
            remote(seg(k, ry, c), seg(k, ry, c), ss.at[HY, k], rs.at[SY, k], to_s),
        ]

    def c_dia(k):
        (a0, an), (b0, bn) = halves(k)
        out = []
        if an:
            out.append(remote(seg(k, ry, cx, a0, an), seg(k, ry, cx, a0, an), ss.at[HD, k], rs.at[SD, k], to_s))
        if bn:
            out.append(remote(seg(k, ry, cx, b0, bn), seg(k, ry, cx, b0, bn), ss.at[HE, k], rs.at[SE, k], to_s))
        return out

    def arrive(dst, sem):
        pltpu.make_async_copy(dst, dst, sem).wait()

    def wait_first(k):
        arrive(seg(k, r, cx), rs.at[FX, k])
        arrive(seg(k, ry, c), rs.at[FY, k])

    def wait_dia(k):
        (a0, an), (b0, bn) = halves(k)
        if an:
            arrive(seg(k, ry, cx, a0, an), rs.at[DY, k])
        if bn:
            arrive(seg(k, ry, cx, b0, bn), rs.at[DX, k])

    def wait_sib(k):
        arrive(seg(k, r, c), rs.at[LO, k])
        arrive(seg(k, r, cs), rs.at[SO, k])
        arrive(seg(k, r, csx), rs.at[SX, k])
        arrive(seg(k, ry, cs), rs.at[SY, k])
        (a0, an), (b0, bn) = halves(k)
        if an:
            arrive(seg(k, ry, csx, a0, an), rs.at[SD, k])
        if bn:
            arrive(seg(k, ry, csx, b0, bn), rs.at[SE, k])

    def start_own(k):
        for cp in c_own(k):
            cp.start()
        c_loc(k).start()

    def at_step(k, fn, lo, hi):
        for kk in range(lo, hi + 1):
            @pl.when(k == kk)
            def _(kk=kk):
                fn(kk)

    t_copies = [
        remote(tp_ref, tl.at[:, c], ts.at[0], ts.at[1], to_x),
        remote(tp_ref, tl.at[:, c], ts.at[2], ts.at[3], to_s),
    ]
    t_on = remote(tl.at[:, cx], tl.at[:, cx], ts.at[4], ts.at[5], to_s)
    t_loc = pltpu.make_async_copy(tp_ref, tl.at[:, c], ts.at[6])
    z_loc = pltpu.make_async_copy(z_ref, xt, zs.at[0])

    start_own(1)
    for cp in t_copies:
        cp.start()
    t_loc.start()
    z_loc.start()
    start_own(2)
    wait_first(1)
    for cp in c_fwd(1) + c_sib(1):
        cp.start()
    arrive(tl.at[:, cx], ts.at[1])
    t_on.start()
    arrive(tl.at[:, cs], ts.at[3])
    arrive(tl.at[:, csx], ts.at[5])
    t_loc.wait()
    z_loc.wait()

    lane = lax.broadcasted_iota(jnp.int32, (128, 128), 1)
    sub = lax.broadcasted_iota(jnp.int32, (128, 128), 0)
    pr, pc = sub // 32, lane // 32
    level1 = (pr // 2 == pc // 2) & (pr < pc)
    level2 = pr // 2 < pc // 2

    def step(k, carry):
        def ahead(kk):
            if kk + 2 <= STEPS:
                start_own(kk + 2)
            if kk + 1 <= STEPS:
                wait_first(kk + 1)
                for cp in c_fwd(kk + 1) + c_sib(kk + 1):
                    cp.start()
            wait_dia(kk)
            for cp in c_dia(kk):
                cp.start()
            wait_sib(kk)

        at_step(k, ahead, 1, STEPS)

        J = STEPS - k
        off = k * (k - 1) // 2
        acc[...] = jnp.zeros_like(acc)

        def tile(m, carry):
            v = jnp.concatenate([land[off + m, 0].reshape(256, 128), land[off + m, 1].reshape(256, 128)], axis=1)
            x = jnp.concatenate([xt[0, J + m], xt[1, J + m]], axis=1)
            vs = split3(v)
            for i in range(3):
                vp[i, m] = vs[i]
            lhs = [jnp.concatenate([a, b], axis=0) for a, b in zip(split3(x), vs)]
            acc[...] += mul6(lhs, vs, NT)
            return carry

        lax.fori_loop(0, k, tile, 0)

        q, h = J // 2, lax.rem(J, 2)

        def diag(tt):
            rows = []
            for cc in range(4):
                t32 = tl[q, cc]
                t32 = jnp.where(h == 0, t32, pltpu.roll(t32, 64, 1))
                shift = (32 * cc - 32 * tt) % 128
                rows.append(pltpu.roll(t32, shift, 1) if shift else t32)
            full = jnp.concatenate(rows, axis=0)
            return jnp.where(pr == pc, full, 0.0)

        halves_t = []
        for tt in range(2):
            g = acc[128 + 128 * tt : 256 + 128 * tt, 128 * tt : 128 * tt + 128]
            t = diag(tt)
            t = t - mulf(t, mulf(jnp.where(level1, g, 0.0), t))
            t = t - mulf(t, mulf(jnp.where(level2, g, 0.0), t))
            halves_t.append(t)
        t1, t2 = halves_t
        t12 = -mulf(t1, mulf(acc[128:256, 128:256], t2))
        w1, w2 = acc[0:128, 0:128], acc[0:128, 128:256]
        w2s = split3(w2)
        y1 = mul6(split3(w1), split3(t1), NT) + mul6(w2s, split3(t12), NT)
        y2 = mul6(w2s, split3(t2), NT)
        ys = split3(jnp.concatenate([y1, y2], axis=1))
        for i in range(3):
            yp[i] = ys[i]

        def send(m):
            return remote(xt.at[ry, m], out_ref.at[r, m], os.at[0], os.at[1], to_y)

        def update(m, carry):
            d = mul6([yp[i] for i in range(3)], [vp[i, m] for i in range(3)], NN)
            xt[0, J + m] = xt[0, J + m] - d[:, :128]
            xt[1, J + m] = xt[1, J + m] - d[:, 128:]

            @pl.when((k == STEPS) & (m > 0))
            def _():
                send(m - 1).start()

            return carry

        lax.fori_loop(0, k, update, 0)
        return carry

    lax.fori_loop(1, STEPS + 1, step, 0)

    o_loc = pltpu.make_async_copy(xt.at[r], out_ref.at[r], os.at[2])
    last = remote(xt.at[ry, STEPS - 1], out_ref.at[r, STEPS - 1], os.at[0], os.at[1], to_y)

    for cp in t_copies:
        cp.wait_send()
    t_on.wait_send()
    for k in range(1, STEPS + 1):
        for cp in c_own(k) + c_fwd(k) + c_sib(k) + c_dia(k):
            cp.wait_send()
    last.start()
    o_loc.start()
    o_loc.wait()
    whole = remote(xt.at[ry], out_ref.at[r], os.at[0], os.at[1], to_y)
    whole.wait_send()
    arrive(out_ref.at[ry], os.at[1])


def solution(mesh):
    def body(v_loc, t_loc, z_loc):
        vt = jnp.transpose(v_loc.reshape(16, 128, 1024), (0, 2, 1)).reshape(16, 32, 32, 128)
        tp = jnp.transpose(t_loc.reshape(8, 4, 32, 32), (0, 2, 1, 3)).reshape(8, 32, 128)
        zt = jnp.transpose(z_loc.reshape(2, 16, 128, 128), (0, 1, 3, 2))
        out = pl.pallas_call(
            kernel,
            out_shape=jax.ShapeDtypeStruct((2, 16, 128, 128), F32),
            in_specs=[pl.BlockSpec(memory_space=pl.ANY)] * 3,
            out_specs=pl.BlockSpec(memory_space=pl.ANY),
            scratch_shapes=[
                pltpu.VMEM((OFF[STEPS + 1], 2, 2, 4, 32, 128), F32),
                pltpu.VMEM((8, 4, 32, 128), F32),
                pltpu.VMEM((2, 16, 128, 128), F32),
                pltpu.VMEM((3, 16, 256, 256), BF16),
                pltpu.VMEM((384, 256), F32),
                pltpu.VMEM((3, 128, 256), BF16),
                pltpu.SemaphoreType.DMA((10, STEPS + 1)),
                pltpu.SemaphoreType.DMA((9, STEPS + 1)),
                pltpu.SemaphoreType.DMA((7,)),
                pltpu.SemaphoreType.DMA((1,)),
                pltpu.SemaphoreType.DMA((3,)),
            ],
            compiler_params=pltpu.CompilerParams(
                collective_id=0, has_side_effects=True, vmem_limit_bytes=64 * 1024 * 1024 - 65536
            ),
        )(vt, tp, zt)
        return jnp.transpose(out, (1, 3, 0, 2)).reshape(2048, 256)

    return jax.shard_map(
        body,
        mesh=mesh,
        in_specs=(P("row", "col"), P("col", None, None), P(None, ("col", "row"))),
        out_specs=P("row", "col"),
        check_vma=False,
    )
```

time: 6260 us -> 246 us (0.04)
  waiting for transfers between devices: 3930 us -> 0 us
  blocking collectives: 1090 us -> 0 us
  matrix products: 859 us -> 0 us
  other arithmetic: 325 us -> 0 us
  Pallas kernels: 0 us -> 227 us
    psum x128 -> x0, waiting for transfers between devices: 3930 us -> none  [panel_step(): v_pan = lax.psum(jnp.where(my_col == owner_col, v_blk, 0.0), 'col')]
    psum x128 -> x0, blocking collectives: 1060 us -> none  [panel_step(): w_full = lax.psum(w_part, 'row')]
    dot_general x384 -> x0, matrix products: 859 us -> none  [the longest x128 405 us: panel_step(): jnp.einsum('nb,nk->bk', v_pan, x_cur, preferred_element_type=jnp.float32,...]
    select_n x128 -> x0, other arithmetic: 325 us -> none  [panel_step(): v_pan = lax.psum(jnp.where(my_col == owner_col, v_blk, 0.0), 'col')]
    pallas_call x0 -> x1, Pallas kernels: none -> 227 us  [body(): pl.pallas_call(kernel, out_shape=jax.ShapeDtypeStruct((2, 16, 128, 128),...]
  transfers between devices with their start and end apart: 129 -> 0, of which waited for: 129 -> 0; matrix products, arithmetic and copies ran while one was open for 0% -> 0% of each run, Pallas kernels for 0% -> 0%
where the time goes in v1:
time: 246 us
  Pallas kernels  227 us (92%)
  local copies, waits for them, and re-layouts  18.8 us (8%)
    pallas_call x1, Pallas kernels, body(): pl.pallas_call(kernel, out_shape=jax.ShapeDtypeStruct((2, 16, 128, 128),...  227 us
    reshape x1, local copies, waits for them, and re-layouts, body(): v_loc.reshape(16, 128, 1024)  9.26 us

profile of v1, /device:TPU:0, one launch (start us, length us, event | category | flops | bytes accessed | tf_op | source)
XLA Modules:
  0.0 245.9 jit_solution(17091432454990907970)
XLA Ops:
  0.0 1.4 copy.17
  1.4 0.9 reshape.21.tp_ref
  2.3 2.9 %copy.8 = f32[2,16,128,128]{2,3,1,0:T(8,128)} copy(f32[2,16,128,128]{3,2,1,0:T(8,128)} %bitcast.22) | data formatting | bytes 4194304 | tf_op jit(solution)/shard_map/reshape | solution.py:269
  5.2 9.3 %copy.6 = f32[16,128,1024]{1,2,0:T(8,128)} copy(f32[16,128,1024]{2,1,0:T(8,128)} %bitcast.19) | data formatting | bytes 16777216 | tf_op jit(solution)/shard_map/reshape | solution.py:267
  14.4 227.1 %shard_map.37 = f32[2,16,128,128]{3,2,1,0:T(8,128)} custom-call(f32[16,32,32,128]{3,2,1,0:T(8,128)} %bitcast.16, f32[8,32,128]{2,1,0:T(8,128)} %reshape.21.tp_ref, f32[2,16,128,128]{3,2,1,0:T(8,128)} %bitcast.18), custom_call_target="tpu_custom_call" | custom-call | tf_op jit(solution)/shard_map/pallas_call | solution.py:270
  241.5 2.9 %copy.11 = f32[16,128,2,128]{3,2,1,0:T(2,128)S(1)} copy(f32[16,128,2,128]{1,3,0,2:T(8,128)} %bitcast.17) | data formatting | bytes 4194304 | tf_op jit(solution)/shard_map/reshape | solution.py:292
  244.4 1.5 copy.16

commit v2 on v1

--- a/solution.py
+++ b/solution.py
@@ -13,6 +13,25 @@
 OFF = [k * (k - 1) // 2 for k in range(STEPS + 2)]
 NT = (((1,), (1,)), ((), ()))
 NN = (((1,), (0,)), ((), ()))
+SWAP = 13
+REST = STEPS - SWAP
+O, F, D, S, T, X = range(6)
+BEFORE = {
+    1: ((O, 1), (T, 0), (O, 2), (F, 1), (O, 3), (F, 2), (O, 4), (D, 1), (S, 1)),
+    2: ((S, 2),),
+    3: ((F, 5), (D, 3), (D, 4), (S, 3)),
+    4: ((S, 4),),
+    5: ((D, 5), (S, 5), (O, 8)),
+    6: ((D, 6), (S, 6), (O, 9)),
+    7: ((D, 7), (S, 7)),
+}
+BEFORE |= {k: ((F, k + 1), (D, k), (S, k)) for k in range(8, 16)}
+BEFORE[16] = ((D, 16), (S, 16))
+MIDDLE = {1: ((O, 5),), 2: ((F, 4), (O, 6)), 3: ((O, 7),)}
+MIDDLE |= {k: ((O, k + 3),) for k in range(7, 14)}
+MIDDLE[14] = ((X, 0),)
+AFTER = {1: ((F, 3), (D, 2)), 4: ((F, 6),), 5: ((F, 7),), 6: ((F, 8),)}
+ALONG_Y = [0, 0, 1, 1, 2, 2, 3, 3, 4, 4, 5, 5, 6, 6, 7, 0, 0]
 FX, FY, DX, DY, SO, SX, SY, SD, SE, LO = range(10)
 TX, TY, TS, GX, GY, HX, HY, HD, HE = range(9)
 
@@ -36,7 +55,7 @@
     return mul6(split3(a), split3(b), dims)
 
 
-def kernel(vt_ref, tp_ref, z_ref, out_ref, land, tl, xt, vp, acc, yp, rs, ss, ts, zs, os):
+def kernel(vt_ref, tp_ref, z_ref, out_ref, land, tl, xt, xs, xn, yo, yn, vp, acc, yp, rs, ss, ts, zs, os, ys):
     r, c = lax.axis_index("row"), lax.axis_index("col")
     cs = c + 1 - 2 * lax.rem(c, 2)
     cx = lax.rem(c + 2, 4)
@@ -61,9 +80,7 @@
         return vt_ref.at[pl.ds(STEPS - k, k), pl.ds(2 * (STEPS - k), 2)]
 
     def halves(k):
-        h = (k + 1) // 2 if k % 2 else k // 2
-        if k % 4 == 1:
-            h = k // 2
+        h = ALONG_Y[k]
         return (0, h), (h, k - h)
 
     def c_own(k):
@@ -130,12 +147,6 @@
             cp.start()
         c_loc(k).start()
 
-    def at_step(k, fn, lo, hi):
-        for kk in range(lo, hi + 1):
-            @pl.when(k == kk)
-            def _(kk=kk):
-                fn(kk)
-
     t_copies = [
         remote(tp_ref, tl.at[:, c], ts.at[0], ts.at[1], to_x),
         remote(tp_ref, tl.at[:, c], ts.at[2], ts.at[3], to_s),
@@ -144,21 +155,48 @@
     t_loc = pltpu.make_async_copy(tp_ref, tl.at[:, c], ts.at[6])
     z_loc = pltpu.make_async_copy(z_ref, xt, zs.at[0])
 
-    start_own(1)
-    for cp in t_copies:
-        cp.start()
-    t_loc.start()
-    z_loc.start()
-    start_own(2)
-    wait_first(1)
-    for cp in c_fwd(1) + c_sib(1):
-        cp.start()
-    arrive(tl.at[:, cx], ts.at[1])
-    t_on.start()
-    arrive(tl.at[:, cs], ts.at[3])
-    arrive(tl.at[:, csx], ts.at[5])
-    t_loc.wait()
-    z_loc.wait()
+    x_copy = remote(xs, xn, os.at[0], os.at[1], to_y)
+
+    def y_copy(i):
+        return remote(yo.at[i], yn.at[i], ys.at[0, i], ys.at[1, i], to_y)
+
+    def do(ops):
+        for op, k in ops:
+            if op == O:
+                start_own(k)
+            elif op == F:
+                wait_first(k)
+                for cp in c_fwd(k) + c_sib(k):
+                    cp.start()
+                if k == 1:
+                    arrive(tl.at[:, cx], ts.at[1])
+                    t_on.start()
+            elif op == D:
+                wait_dia(k)
+                for cp in c_dia(k):
+                    cp.start()
+            elif op == S:
+                wait_sib(k)
+                if k == 1:
+                    arrive(tl.at[:, cs], ts.at[3])
+                    arrive(tl.at[:, csx], ts.at[5])
+                    t_loc.wait()
+                    z_loc.wait()
+                if k > SWAP + 1:
+                    y_copy(k - SWAP - 2).start()
+            elif op == T:
+                for cp in t_copies:
+                    cp.start()
+                t_loc.start()
+                z_loc.start()
+            else:
+                x_copy.start()
+
+    def point(k, table):
+        for kk, ops in table.items():
+            @pl.when(k == kk)
+            def _(ops=ops):
+                do(ops)
 
     lane = lax.broadcasted_iota(jnp.int32, (128, 128), 1)
     sub = lax.broadcasted_iota(jnp.int32, (128, 128), 0)
@@ -167,20 +205,7 @@
     level2 = pr // 2 < pc // 2
 
     def step(k, carry):
-        def ahead(kk):
-            if kk + 2 <= STEPS:
-                start_own(kk + 2)
-            if kk + 1 <= STEPS:
-                wait_first(kk + 1)
-                for cp in c_fwd(kk + 1) + c_sib(kk + 1):
-                    cp.start()
-            wait_dia(kk)
-            for cp in c_dia(kk):
-                cp.start()
-            wait_sib(kk)
-
-        at_step(k, ahead, 1, STEPS)
-
+        point(k, BEFORE)
         J = STEPS - k
         off = k * (k - 1) // 2
         acc[...] = jnp.zeros_like(acc)
@@ -195,7 +220,10 @@
             acc[...] += mul6(lhs, vs, NT)
             return carry
 
-        lax.fori_loop(0, k, tile, 0)
+        mid = lax.div(k + 1, 2)
+        lax.fori_loop(0, mid, tile, 0)
+        point(k, MIDDLE)
+        lax.fori_loop(mid, k, tile, 0)
 
         q, h = J // 2, lax.rem(J, 2)
 
@@ -222,31 +250,58 @@
         w2s = split3(w2)
         y1 = mul6(split3(w1), split3(t1), NT) + mul6(w2s, split3(t12), NT)
         y2 = mul6(w2s, split3(t2), NT)
-        ys = split3(jnp.concatenate([y1, y2], axis=1))
-        for i in range(3):
-            yp[i] = ys[i]
-
-        def send(m):
-            return remote(xt.at[ry, m], out_ref.at[r, m], os.at[0], os.at[1], to_y)
+        y = jnp.concatenate([y1, y2], axis=1)
+        for i, part in enumerate(split3(y)):
+            yp[i] = part
+
+        @pl.when(k > SWAP)
+        def _():
+            yo[k - SWAP - 1] = y
+
+        point(k, AFTER)
 
         def update(m, carry):
             d = mul6([yp[i] for i in range(3)], [vp[i, m] for i in range(3)], NN)
             xt[0, J + m] = xt[0, J + m] - d[:, :128]
             xt[1, J + m] = xt[1, J + m] - d[:, 128:]
-
-            @pl.when((k == STEPS) & (m > 0))
-            def _():
-                send(m - 1).start()
-
             return carry
 
-        lax.fori_loop(0, k, update, 0)
+        @pl.when(k < STEPS)
+        def _():
+            lax.fori_loop(0, k, update, 0)
+
+        @pl.when(k == SWAP)
+        def _():
+            def stage(m, carry):
+                xs[m] = xt[ry, m]
+                return carry
+
+            lax.fori_loop(0, STEPS, stage, 0)
+
         return carry
 
     lax.fori_loop(1, STEPS + 1, step, 0)
 
+    def half(dst, k, parts, lo, hi):
+        def tile(m, carry):
+            v = split3(land[OFF[k] + m, r].reshape(256, 128))
+            dst[STEPS - k + m] = dst[STEPS - k + m] - mul6(parts, v, NN)
+            return carry
+
+        lax.fori_loop(lo, hi, tile, 0)
+
+    last = [yp[i] for i in range(3)]
+    half(xt.at[r], STEPS, last, 0, 4)
+    y_copy(REST - 1).start()
+    half(xt.at[r], STEPS, last, 4, STEPS)
     o_loc = pltpu.make_async_copy(xt.at[r], out_ref.at[r], os.at[2])
-    last = remote(xt.at[ry, STEPS - 1], out_ref.at[r, STEPS - 1], os.at[0], os.at[1], to_y)
+    o_loc.start()
+    arrive(xn, os.at[1])
+    for i in range(REST):
+        arrive(yn.at[i], ys.at[1, i])
+        half(xn, SWAP + 1 + i, split3(yn[i]), 0, SWAP + 1 + i)
+    o_nbr = pltpu.make_async_copy(xn, out_ref.at[ry], os.at[3])
+    o_nbr.start()
 
     for cp in t_copies:
         cp.wait_send()
@@ -254,12 +309,11 @@
     for k in range(1, STEPS + 1):
         for cp in c_own(k) + c_fwd(k) + c_sib(k) + c_dia(k):
             cp.wait_send()
-    last.start()
-    o_loc.start()
+    x_copy.wait_send()
+    for i in range(REST):
+        y_copy(i).wait_send()
     o_loc.wait()
-    whole = remote(xt.at[ry], out_ref.at[r], os.at[0], os.at[1], to_y)
-    whole.wait_send()
-    arrive(out_ref.at[ry], os.at[1])
+    o_nbr.wait()
 
 
 def solution(mesh):
@@ -276,6 +330,10 @@
                 pltpu.VMEM((OFF[STEPS + 1], 2, 2, 4, 32, 128), F32),
                 pltpu.VMEM((8, 4, 32, 128), F32),
                 pltpu.VMEM((2, 16, 128, 128), F32),
+                pltpu.VMEM((16, 128, 128), F32),
+                pltpu.VMEM((16, 128, 128), F32),
+                pltpu.VMEM((REST, 128, 256), F32),
+                pltpu.VMEM((REST, 128, 256), F32),
                 pltpu.VMEM((3, 16, 256, 256), BF16),
                 pltpu.VMEM((384, 256), F32),
                 pltpu.VMEM((3, 128, 256), BF16),
@@ -283,7 +341,8 @@
                 pltpu.SemaphoreType.DMA((9, STEPS + 1)),
                 pltpu.SemaphoreType.DMA((7,)),
                 pltpu.SemaphoreType.DMA((1,)),
-                pltpu.SemaphoreType.DMA((3,)),
+                pltpu.SemaphoreType.DMA((4,)),
+                pltpu.SemaphoreType.DMA((2, REST)),
             ],
             compiler_params=pltpu.CompilerParams(
                 collective_id=0, has_side_effects=True, vmem_limit_bytes=64 * 1024 * 1024 - 65536

time: 246 us -> 233 us (0.947)
  Pallas kernels: 227 us -> 214 us
    pallas_call x1, Pallas kernels: 227 us -> 214 us  [body(): pl.pallas_call(kernel, out_shape=jax.ShapeDtypeStruct((2, 16, 128, 128),...]
where the time goes in v2:
time: 233 us; the launch traced here: 232 us
  Pallas kernels  214 us (92%)
  local copies, waits for them, and re-layouts  18.8 us (8%)
    pallas_call x1, Pallas kernels, body(): pl.pallas_call(kernel, out_shape=jax.ShapeDtypeStruct((2, 16, 128, 128),...  214 us
    reshape x1, local copies, waits for them, and re-layouts, body(): v_loc.reshape(16, 128, 1024)  9.26 us

profile of v2, /device:TPU:0, one launch (start us, length us, event | category | flops | bytes accessed | tf_op | source)
XLA Modules:
  0.0 232.4 jit_solution(3744009724024787527)
XLA Ops:
  0.0 1.4 copy.17
  1.4 0.9 reshape.21.tp_ref
  2.3 2.9 %copy.8 = f32[2,16,128,128]{2,3,1,0:T(8,128)} copy(f32[2,16,128,128]{3,2,1,0:T(8,128)} %bitcast.22) | data formatting | bytes 4194304 | tf_op jit(solution)/shard_map/reshape | solution.py:323
  5.2 9.3 %copy.6 = f32[16,128,1024]{1,2,0:T(8,128)} copy(f32[16,128,1024]{2,1,0:T(8,128)} %bitcast.19) | data formatting | bytes 16777216 | tf_op jit(solution)/shard_map/reshape | solution.py:321
  14.4 213.5 %shard_map.37 = f32[2,16,128,128]{3,2,1,0:T(8,128)} custom-call(f32[16,32,32,128]{3,2,1,0:T(8,128)} %bitcast.16, f32[8,32,128]{2,1,0:T(8,128)} %reshape.21.tp_ref, f32[2,16,128,128]{3,2,1,0:T(8,128)} %bitcast.18), custom_call_target="tpu_custom_call" | custom-call | tf_op jit(solution)/shard_map/pallas_call | solution.py:324
  228.0 2.9 %copy.11 = f32[16,128,2,128]{3,2,1,0:T(2,128)S(1)} copy(f32[16,128,2,128]{1,3,0,2:T(8,128)} %bitcast.17) | data formatting | bytes 4194304 | tf_op jit(solution)/shard_map/reshape | solution.py:351
  230.9 1.5 copy.16

commit v3 on v2

--- a/solution.py
+++ b/solution.py
@@ -63,13 +63,12 @@
     ry = 1 - r
     to_x, to_y, to_s = (r, cx), (ry, c), (r, cs)
 
-    barrier = pltpu.get_barrier_semaphore()
-    for dev in (to_x, to_y, to_s):
-        pl.semaphore_signal(barrier, inc=1, device_id=dev, device_id_type=MESH)
-    pl.semaphore_wait(barrier, 3)
-
     def seg(k, rr, cc, lo=0, n=None):
-        return land.at[pl.ds(OFF[k] + lo, k if n is None else n), rr, :, cc]
+        return land.at[pl.ds(8 * OFF[k] + (rr * 4 + cc) * k + lo, k if n is None else n)]
+
+    def rows(k, base, rr, m):
+        got = [land[base + (rr * 4 + cc) * k + m] for cc in range(4)]
+        return jnp.concatenate([g[:32] for g in got] + [g[32:] for g in got], axis=0)
 
     def remote(src, dst, send, recv, dev):
         return pltpu.make_async_remote_copy(
@@ -77,17 +76,18 @@
         )
 
     def own(k):
-        return vt_ref.at[pl.ds(STEPS - k, k), pl.ds(2 * (STEPS - k), 2)]
+        return vt_ref.at[pl.ds(STEPS - k, k), STEPS - k]
 
     def halves(k):
         h = ALONG_Y[k]
         return (0, h), (h, k - h)
 
     def c_own(k):
+        mine = seg(k, r, c)
         return [
-            remote(own(k), seg(k, r, c), ss.at[TX, k], rs.at[FX, k], to_x),
-            remote(own(k), seg(k, r, c), ss.at[TY, k], rs.at[FY, k], to_y),
-            remote(own(k), seg(k, r, c), ss.at[TS, k], rs.at[SO, k], to_s),
+            remote(mine, mine, ss.at[TX, k], rs.at[FX, k], to_x),
+            remote(mine, mine, ss.at[TY, k], rs.at[FY, k], to_y),
+            remote(mine, mine, ss.at[TS, k], rs.at[SO, k], to_s),
         ]
 
     def c_loc(k):
@@ -132,7 +132,6 @@
             arrive(seg(k, ry, cx, b0, bn), rs.at[DX, k])
 
     def wait_sib(k):
-        arrive(seg(k, r, c), rs.at[LO, k])
         arrive(seg(k, r, cs), rs.at[SO, k])
         arrive(seg(k, r, csx), rs.at[SX, k])
         arrive(seg(k, ry, cs), rs.at[SY, k])
@@ -143,9 +142,16 @@
             arrive(seg(k, ry, csx, b0, bn), rs.at[SE, k])
 
     def start_own(k):
+        c_loc(k).wait()
         for cp in c_own(k):
             cp.start()
+
+    for k in range(1, STEPS + 1):
         c_loc(k).start()
+    barrier = pltpu.get_barrier_semaphore()
+    for dev in (to_x, to_y, to_s):
+        pl.semaphore_signal(barrier, inc=1, device_id=dev, device_id_type=MESH)
+    pl.semaphore_wait(barrier, 3)
 
     t_copies = [
         remote(tp_ref, tl.at[:, c], ts.at[0], ts.at[1], to_x),
@@ -207,11 +213,11 @@
     def step(k, carry):
         point(k, BEFORE)
         J = STEPS - k
-        off = k * (k - 1) // 2
+        base = 4 * k * (k - 1)
         acc[...] = jnp.zeros_like(acc)
 
         def tile(m, carry):
-            v = jnp.concatenate([land[off + m, 0].reshape(256, 128), land[off + m, 1].reshape(256, 128)], axis=1)
+            v = jnp.concatenate([rows(k, base, 0, m), rows(k, base, 1, m)], axis=1)
             x = jnp.concatenate([xt[0, J + m], xt[1, J + m]], axis=1)
             vs = split3(v)
             for i in range(3):
@@ -284,7 +290,7 @@
 
     def half(dst, k, parts, lo, hi):
         def tile(m, carry):
-            v = split3(land[OFF[k] + m, r].reshape(256, 128))
+            v = split3(rows(k, 8 * OFF[k], r, m))
             dst[STEPS - k + m] = dst[STEPS - k + m] - mul6(parts, v, NN)
             return carry
 
@@ -318,7 +324,7 @@
 
 def solution(mesh):
     def body(v_loc, t_loc, z_loc):
-        vt = jnp.transpose(v_loc.reshape(16, 128, 1024), (0, 2, 1)).reshape(16, 32, 32, 128)
+        vt = jnp.transpose(v_loc.reshape(16, 128, 1024), (0, 2, 1)).reshape(16, 16, 64, 128)
         tp = jnp.transpose(t_loc.reshape(8, 4, 32, 32), (0, 2, 1, 3)).reshape(8, 32, 128)
         zt = jnp.transpose(z_loc.reshape(2, 16, 128, 128), (0, 1, 3, 2))
         out = pl.pallas_call(
@@ -327,7 +333,7 @@
             in_specs=[pl.BlockSpec(memory_space=pl.ANY)] * 3,
             out_specs=pl.BlockSpec(memory_space=pl.ANY),
             scratch_shapes=[
-                pltpu.VMEM((OFF[STEPS + 1], 2, 2, 4, 32, 128), F32),
+                pltpu.VMEM((8 * OFF[STEPS + 1], 64, 128), F32),
                 pltpu.VMEM((8, 4, 32, 128), F32),
                 pltpu.VMEM((2, 16, 128, 128), F32),
                 pltpu.VMEM((16, 128, 128), F32),

time: 233 us -> 229 us (0.983)
  Pallas kernels: 214 us -> 210 us
    pallas_call x1, Pallas kernels: 214 us -> 210 us  [body(): pl.pallas_call(kernel, out_shape=jax.ShapeDtypeStruct((2, 16, 128, 128),...]
where the time goes in v3:
time: 229 us
  Pallas kernels  210 us (92%)
  local copies, waits for them, and re-layouts  18.8 us (8%)
    pallas_call x1, Pallas kernels, body(): pl.pallas_call(kernel, out_shape=jax.ShapeDtypeStruct((2, 16, 128, 128),...  210 us
    reshape x1, local copies, waits for them, and re-layouts, body(): v_loc.reshape(16, 128, 1024)  9.26 us

profile of v3, /device:TPU:0, one launch (start us, length us, event | category | flops | bytes accessed | tf_op | source)
XLA Modules:
  0.0 229.0 jit_solution(8214253156016947603)
XLA Ops:
  0.0 1.4 copy.17
  1.4 0.9 reshape.21.tp_ref
  2.3 2.9 %copy.8 = f32[2,16,128,128]{2,3,1,0:T(8,128)} copy(f32[2,16,128,128]{3,2,1,0:T(8,128)} %bitcast.22) | data formatting | bytes 4194304 | tf_op jit(solution)/shard_map/reshape | solution.py:329
  5.2 9.3 %copy.6 = f32[16,128,1024]{1,2,0:T(8,128)} copy(f32[16,128,1024]{2,1,0:T(8,128)} %bitcast.19) | data formatting | bytes 16777216 | tf_op jit(solution)/shard_map/reshape | solution.py:327
  14.4 210.2 %shard_map.37 = f32[2,16,128,128]{3,2,1,0:T(8,128)} custom-call(f32[16,16,64,128]{3,2,1,0:T(8,128)} %bitcast.16, f32[8,32,128]{2,1,0:T(8,128)} %reshape.21.tp_ref, f32[2,16,128,128]{3,2,1,0:T(8,128)} %bitcast.18), custom_call_target="tpu_custom_call" | custom-call | tf_op jit(solution)/shard_map/pallas_call | solution.py:330
  224.6 2.9 %copy.11 = f32[16,128,2,128]{3,2,1,0:T(2,128)S(1)} copy(f32[16,128,2,128]{1,3,0,2:T(8,128)} %bitcast.17) | data formatting | bytes 4194304 | tf_op jit(solution)/shard_map/reshape | solution.py:357
  227.6 1.5 copy.16

commit v4 on v3

--- a/solution.py
+++ b/solution.py
@@ -90,6 +90,19 @@
             remote(mine, mine, ss.at[TS, k], rs.at[SO, k], to_s),
         ]
 
+    def c_own_start(k):
+        if k < 2:
+            return c_own(k)
+        h = k // 2
+        a, b = seg(k, r, c, 0, h), seg(k, r, c, h, k - h)
+        return [
+            remote(a, a, ss.at[TX, k], rs.at[FX, k], to_x),
+            remote(a, a, ss.at[TY, k], rs.at[FY, k], to_y),
+            remote(b, b, ss.at[TX, k], rs.at[FX, k], to_x),
+            remote(b, b, ss.at[TY, k], rs.at[FY, k], to_y),
+            c_own(k)[2],
+        ]
+
     def c_loc(k):
         return pltpu.make_async_copy(own(k), seg(k, r, c), rs.at[LO, k])
 
@@ -143,7 +156,7 @@
 
     def start_own(k):
         c_loc(k).wait()
-        for cp in c_own(k):
+        for cp in c_own_start(k):
             cp.start()
 
     for k in range(1, STEPS + 1):

time: 229 us -> 230 us (level)
  no operation moved by 1% of the time
where the time goes in v4:
time: 230 us; the launch traced here: 229 us
  Pallas kernels  210 us (91%)
  local copies, waits for them, and re-layouts  18.8 us (8%)
    pallas_call x1, Pallas kernels, body(): pl.pallas_call(kernel, out_shape=jax.ShapeDtypeStruct((2, 16, 128, 128),...  210 us
    reshape x1, local copies, waits for them, and re-layouts, body(): v_loc.reshape(16, 128, 1024)  9.26 us

profile of v4, /device:TPU:0, one launch (start us, length us, event | category | flops | bytes accessed | tf_op | source)
XLA Modules:
  0.0 229.3 jit_solution(13300007686703677044)
XLA Ops:
  0.0 1.4 copy.17
  1.4 0.9 reshape.21.tp_ref
  2.3 2.9 %copy.8 = f32[2,16,128,128]{2,3,1,0:T(8,128)} copy(f32[2,16,128,128]{3,2,1,0:T(8,128)} %bitcast.22) | data formatting | bytes 4194304 | tf_op jit(solution)/shard_map/reshape | solution.py:342
  5.2 9.3 %copy.6 = f32[16,128,1024]{1,2,0:T(8,128)} copy(f32[16,128,1024]{2,1,0:T(8,128)} %bitcast.19) | data formatting | bytes 16777216 | tf_op jit(solution)/shard_map/reshape | solution.py:340
  14.4 210.4 %shard_map.37 = f32[2,16,128,128]{3,2,1,0:T(8,128)} custom-call(f32[16,16,64,128]{3,2,1,0:T(8,128)} %bitcast.16, f32[8,32,128]{2,1,0:T(8,128)} %reshape.21.tp_ref, f32[2,16,128,128]{3,2,1,0:T(8,128)} %bitcast.18), custom_call_target="tpu_custom_call" | custom-call | tf_op jit(solution)/shard_map/pallas_call | solution.py:343
  224.9 2.9 %copy.11 = f32[16,128,2,128]{3,2,1,0:T(2,128)S(1)} copy(f32[16,128,2,128]{1,3,0,2:T(8,128)} %bitcast.17) | data formatting | bytes 4194304 | tf_op jit(solution)/shard_map/reshape | solution.py:370
  227.8 1.5 copy.16

commit v5 on v3

--- a/solution.py
+++ b/solution.py
@@ -16,21 +16,12 @@
 SWAP = 13
 REST = STEPS - SWAP
 O, F, D, S, T, X = range(6)
-BEFORE = {
-    1: ((O, 1), (T, 0), (O, 2), (F, 1), (O, 3), (F, 2), (O, 4), (D, 1), (S, 1)),
-    2: ((S, 2),),
-    3: ((F, 5), (D, 3), (D, 4), (S, 3)),
-    4: ((S, 4),),
-    5: ((D, 5), (S, 5), (O, 8)),
-    6: ((D, 6), (S, 6), (O, 9)),
-    7: ((D, 7), (S, 7)),
-}
-BEFORE |= {k: ((F, k + 1), (D, k), (S, k)) for k in range(8, 16)}
-BEFORE[16] = ((D, 16), (S, 16))
-MIDDLE = {1: ((O, 5),), 2: ((F, 4), (O, 6)), 3: ((O, 7),)}
-MIDDLE |= {k: ((O, k + 3),) for k in range(7, 14)}
-MIDDLE[14] = ((X, 0),)
-AFTER = {1: ((F, 3), (D, 2)), 4: ((F, 6),), 5: ((F, 7),), 6: ((F, 8),)}
+BEFORE = {k: ((S, k),) for k in range(2, STEPS + 1)}
+BEFORE[1] = ((O, 1), (O, 2), (T, 0), (O, 3), (F, 1), (O, 4), (F, 2), (D, 1), (S, 1))
+MIDDLE = {k: ((F, k + 2), (O, k + 4)) for k in range(1, 13)}
+MIDDLE[13] = ((F, 15),)
+MIDDLE[14] = ((X, 0), (F, 16))
+AFTER = {k: ((D, k + 1),) for k in range(1, 16)}
 ALONG_Y = [0, 0, 1, 1, 2, 2, 3, 3, 4, 4, 5, 5, 6, 6, 7, 0, 0]
 FX, FY, DX, DY, SO, SX, SY, SD, SE, LO = range(10)
 TX, TY, TS, GX, GY, HX, HY, HD, HE = range(9)
@@ -55,7 +46,22 @@
     return mul6(split3(a), split3(b), dims)
 
 
-def kernel(vt_ref, tp_ref, z_ref, out_ref, land, tl, xt, xs, xn, yo, yn, vp, acc, yp, rs, ss, ts, zs, os, ys):
+def by_four(lo, hi, fn):
+    fours = lax.div(hi - lo, 4)
+
+    def four(i, carry):
+        fn(lo + 4 * i, 4)
+        return carry
+
+    def one(m, carry):
+        fn(m, 1)
+        return carry
+
+    lax.fori_loop(0, fours, four, 0)
+    lax.fori_loop(lo + 4 * fours, hi, one, 0)
+
+
+def kernel(vt_ref, tp_ref, z_ref, out_ref, land, tl, xt, xs, xn, yo, yn, vp, lp, acc, yp, rs, ss, ts, zs, os, ys):
     r, c = lax.axis_index("row"), lax.axis_index("col")
     cs = c + 1 - 2 * lax.rem(c, 2)
     cx = lax.rem(c + 2, 4)
@@ -216,20 +222,39 @@
         base = 4 * k * (k - 1)
         acc[...] = jnp.zeros_like(acc)
 
-        def tile(m, carry):
-            v = jnp.concatenate([rows(k, base, 0, m), rows(k, base, 1, m)], axis=1)
-            x = jnp.concatenate([xt[0, J + m], xt[1, J + m]], axis=1)
-            vs = split3(v)
-            for i in range(3):
-                vp[i, m] = vs[i]
-            lhs = [jnp.concatenate([a, b], axis=0) for a, b in zip(split3(x), vs)]
-            acc[...] += mul6(lhs, vs, NT)
+        def prepare(m, p):
+            m = jnp.minimum(m, k - 1)
+            for g in range(12):
+                if g < 4:
+                    here = [xt[rr, J + m, 32 * g : 32 * g + 32] for rr in range(2)]
+                else:
+                    tt, cc = divmod(g - 4, 4)
+                    here = [land[base + (rr * 4 + cc) * k + m, 32 * tt : 32 * tt + 32] for rr in range(2)]
+                for i, part in enumerate(split3(jnp.concatenate(here, axis=1))):
+                    lp[p, i, 32 * g : 32 * g + 32] = part
+                    if g >= 4:
+                        vp[i, m, 32 * g - 128 : 32 * g - 96] = part
+
+        def product(p):
+            return mul6([lp[p, i] for i in range(3)], [lp[p, i, 128:384] for i in range(3)], NT)
+
+        def pair(i, carry):
+            acc[...] += product(0) + product(1)
+            prepare(2 * i + 2, 0)
+            prepare(2 * i + 3, 1)
             return carry
 
-        mid = lax.div(k + 1, 2)
-        lax.fori_loop(0, mid, tile, 0)
+        pairs = lax.div(k, 2)
+        mid = lax.div(pairs + 1, 2)
+        prepare(0, 0)
+        prepare(1, 1)
+        lax.fori_loop(0, mid, pair, 0)
         point(k, MIDDLE)
-        lax.fori_loop(mid, k, tile, 0)
+        lax.fori_loop(mid, pairs, pair, 0)
+
+        @pl.when(lax.rem(k, 2) == 1)
+        def _():
+            acc[...] += product(0)
 
         q, h = J // 2, lax.rem(J, 2)
 
@@ -266,15 +291,16 @@
 
         point(k, AFTER)
 
-        def update(m, carry):
-            d = mul6([yp[i] for i in range(3)], [vp[i, m] for i in range(3)], NN)
-            xt[0, J + m] = xt[0, J + m] - d[:, :128]
-            xt[1, J + m] = xt[1, J + m] - d[:, 128:]
-            return carry
+        def update(m, n):
+            ps = [yp[i] for i in range(3)]
+            ds = [mul6(ps, [vp[i, m + u] for i in range(3)], NN) for u in range(n)]
+            for u, d in enumerate(ds):
+                xt[0, J + m + u] = xt[0, J + m + u] - d[:, :128]
+                xt[1, J + m + u] = xt[1, J + m + u] - d[:, 128:]
 
         @pl.when(k < STEPS)
         def _():
-            lax.fori_loop(0, k, update, 0)
+            by_four(0, k, update)
 
         @pl.when(k == SWAP)
         def _():
@@ -289,12 +315,12 @@
     lax.fori_loop(1, STEPS + 1, step, 0)
 
     def half(dst, k, parts, lo, hi):
-        def tile(m, carry):
-            v = split3(rows(k, 8 * OFF[k], r, m))
-            dst[STEPS - k + m] = dst[STEPS - k + m] - mul6(parts, v, NN)
-            return carry
-
-        lax.fori_loop(lo, hi, tile, 0)
+        def tiles(m, n):
+            ds = [mul6(parts, split3(rows(k, 8 * OFF[k], r, m + u)), NN) for u in range(n)]
+            for u, d in enumerate(ds):
+                dst[STEPS - k + m + u] = dst[STEPS - k + m + u] - d
+
+        by_four(lo, hi, tiles)
 
     last = [yp[i] for i in range(3)]
     half(xt.at[r], STEPS, last, 0, 4)
@@ -341,6 +367,7 @@
                 pltpu.VMEM((REST, 128, 256), F32),
                 pltpu.VMEM((REST, 128, 256), F32),
                 pltpu.VMEM((3, 16, 256, 256), BF16),
+                pltpu.VMEM((2, 3, 384, 256), BF16),
                 pltpu.VMEM((384, 256), F32),
                 pltpu.VMEM((3, 128, 256), BF16),
                 pltpu.SemaphoreType.DMA((10, STEPS + 1)),

time: 229 us -> 211 us (0.921)
  Pallas kernels: 210 us -> 192 us
    pallas_call x1, Pallas kernels: 210 us -> 192 us  [body(): pl.pallas_call(kernel, out_shape=jax.ShapeDtypeStruct((2, 16, 128, 128),...]
where the time goes in v5:
time: 211 us
  Pallas kernels  192 us (91%)
  local copies, waits for them, and re-layouts  18.8 us (9%)
    pallas_call x1, Pallas kernels, body(): pl.pallas_call(kernel, out_shape=jax.ShapeDtypeStruct((2, 16, 128, 128),...  192 us
    reshape x1, local copies, waits for them, and re-layouts, body(): v_loc.reshape(16, 128, 1024)  9.26 us

profile of v5, /device:TPU:0, one launch (start us, length us, event | category | flops | bytes accessed | tf_op | source)
XLA Modules:
  0.0 211.1 jit_solution(12383215712989510666)
XLA Ops:
  0.0 1.4 copy.17
  1.4 0.9 reshape.21.tp_ref
  2.3 2.9 %copy.8 = f32[2,16,128,128]{2,3,1,0:T(8,128)} copy(f32[2,16,128,128]{3,2,1,0:T(8,128)} %bitcast.22) | data formatting | bytes 4194304 | tf_op jit(solution)/shard_map/reshape | solution.py:355
  5.2 9.3 %copy.6 = f32[16,128,1024]{1,2,0:T(8,128)} copy(f32[16,128,1024]{2,1,0:T(8,128)} %bitcast.19) | data formatting | bytes 16777216 | tf_op jit(solution)/shard_map/reshape | solution.py:353
  14.4 192.3 %shard_map.37 = f32[2,16,128,128]{3,2,1,0:T(8,128)} custom-call(f32[16,16,64,128]{3,2,1,0:T(8,128)} %bitcast.16, f32[8,32,128]{2,1,0:T(8,128)} %reshape.21.tp_ref, f32[2,16,128,128]{3,2,1,0:T(8,128)} %bitcast.18), custom_call_target="tpu_custom_call" | custom-call | tf_op jit(solution)/shard_map/pallas_call | solution.py:356
  206.7 2.9 %copy.11 = f32[16,128,2,128]{3,2,1,0:T(2,128)S(1)} copy(f32[16,128,2,128]{1,3,0,2:T(8,128)} %bitcast.17) | data formatting | bytes 4194304 | tf_op jit(solution)/shard_map/reshape | solution.py:384
  209.7 1.5 copy.16

commit v6 on v5

--- a/solution.py
+++ b/solution.py
@@ -15,14 +15,17 @@
 NN = (((1,), (0,)), ((), ()))
 SWAP = 13
 REST = STEPS - SWAP
-O, F, D, S, T, X = range(6)
+O, F, D, S, T, X, V = range(7)
 BEFORE = {k: ((S, k),) for k in range(2, STEPS + 1)}
-BEFORE[1] = ((O, 1), (O, 2), (T, 0), (O, 3), (F, 1), (O, 4), (F, 2), (D, 1), (S, 1))
+BEFORE[1] = ((V, 1), (V, 2), (O, 1), (O, 2), (V, 3), (T, 0), (O, 3), (F, 1), (O, 4), (F, 2), (D, 1), (S, 1))
+BEFORE[14] = ((S, 14), (X, 0))
+BEFORE[15] = ((D, 15), (S, 15))
 MIDDLE = {k: ((F, k + 2), (O, k + 4)) for k in range(1, 13)}
+MIDDLE |= {k: MIDDLE[k] + ((V, (k + 7) // 2),) for k in range(1, 10, 2)}
 MIDDLE[13] = ((F, 15),)
-MIDDLE[14] = ((X, 0), (F, 16))
-AFTER = {k: ((D, k + 1),) for k in range(1, 16)}
-ALONG_Y = [0, 0, 1, 1, 2, 2, 3, 3, 4, 4, 5, 5, 6, 6, 7, 0, 0]
+MIDDLE[14] = ((F, 16),)
+AFTER = {k: ((D, k + 1),) for k in (*range(1, 14), 15)}
+ALONG_Y = [0, 0, 1, 1, 2, 2, 3, 3, 4, 4, 5, 5, 6, 6, 7, 7, 0]
 FX, FY, DX, DY, SO, SX, SY, SD, SE, LO = range(10)
 TX, TY, TS, GX, GY, HX, HY, HD, HE = range(9)
 
@@ -61,7 +64,7 @@
     lax.fori_loop(lo + 4 * fours, hi, one, 0)
 
 
-def kernel(vt_ref, tp_ref, z_ref, out_ref, land, tl, xt, xs, xn, yo, yn, vp, lp, acc, yp, rs, ss, ts, zs, os, ys):
+def kernel(v_ref, t_ref, z_ref, out_ref, vs_in, t_in, z_in, ob, land, tl, xt, xs, xn, yo, yn, vp, lp, acc, yp, rs, ss, ts, zs, os, ys):
     r, c = lax.axis_index("row"), lax.axis_index("col")
     cs = c + 1 - 2 * lax.rem(c, 2)
     cx = lax.rem(c + 2, 4)
@@ -80,9 +83,6 @@
         return pltpu.make_async_remote_copy(
             src_ref=src, dst_ref=dst, send_sem=send, recv_sem=recv, device_id=dev, device_id_type=MESH
         )
-
-    def own(k):
-        return vt_ref.at[pl.ds(STEPS - k, k), STEPS - k]
 
     def halves(k):
         h = ALONG_Y[k]
@@ -96,8 +96,27 @@
             remote(mine, mine, ss.at[TS, k], rs.at[SO, k], to_s),
         ]
 
-    def c_loc(k):
-        return pltpu.make_async_copy(own(k), seg(k, r, c), rs.at[LO, k])
+    def c_loc(n):
+        q = STEPS // 2 - n
+        return pltpu.make_async_copy(
+            v_ref.at[pl.ds(256 * q, 256 * n), pl.ds(128 * q, 128)], vs_in.at[pl.ds(256 * OFF[n], 256 * n)], rs.at[LO, n]
+        )
+
+    def turn(n):
+        c_loc(n).wait()
+        even, odd = (8 * OFF[k] + (r * 4 + c) * k for k in (2 * n, 2 * n - 1))
+
+        def tile(m, carry):
+            t = vs_in[pl.ds(pl.multiple_of(256 * OFF[n] + 128 * m, 128), 128)].T
+            land[even + m] = t[:64]
+
+            @pl.when(m > 0)
+            def _():
+                land[odd + m - 1] = t[64:]
+
+            return carry
+
+        lax.fori_loop(0, 2 * n, tile, 0)
 
     def c_fwd(k):
         (a0, an), (b0, bn) = halves(k)
@@ -148,24 +167,26 @@
             arrive(seg(k, ry, csx, b0, bn), rs.at[SE, k])
 
     def start_own(k):
-        c_loc(k).wait()
         for cp in c_own(k):
             cp.start()
 
-    for k in range(1, STEPS + 1):
-        c_loc(k).start()
+    t_loc = pltpu.make_async_copy(t_ref, t_in, ts.at[6])
+    z_loc = pltpu.make_async_copy(z_ref, z_in, zs.at[0])
+    for n in range(1, STEPS // 2 + 1):
+        c_loc(n).start()
+        if n == 2:
+            t_loc.start()
+            z_loc.start()
     barrier = pltpu.get_barrier_semaphore()
     for dev in (to_x, to_y, to_s):
         pl.semaphore_signal(barrier, inc=1, device_id=dev, device_id_type=MESH)
     pl.semaphore_wait(barrier, 3)
 
     t_copies = [
-        remote(tp_ref, tl.at[:, c], ts.at[0], ts.at[1], to_x),
-        remote(tp_ref, tl.at[:, c], ts.at[2], ts.at[3], to_s),
+        remote(tl.at[:, c], tl.at[:, c], ts.at[0], ts.at[1], to_x),
+        remote(tl.at[:, c], tl.at[:, c], ts.at[2], ts.at[3], to_s),
     ]
     t_on = remote(tl.at[:, cx], tl.at[:, cx], ts.at[4], ts.at[5], to_s)
-    t_loc = pltpu.make_async_copy(tp_ref, tl.at[:, c], ts.at[6])
-    z_loc = pltpu.make_async_copy(z_ref, xt, zs.at[0])
 
     x_copy = remote(xs, xn, os.at[0], os.at[1], to_y)
 
@@ -192,15 +213,18 @@
                 if k == 1:
                     arrive(tl.at[:, cs], ts.at[3])
                     arrive(tl.at[:, csx], ts.at[5])
-                    t_loc.wait()
                     z_loc.wait()
                 if k > SWAP + 1:
                     y_copy(k - SWAP - 2).start()
             elif op == T:
                 for cp in t_copies:
                     cp.start()
-                t_loc.start()
-                z_loc.start()
+            elif op == V:
+                turn(k)
+                if k == 2:
+                    t_loc.wait()
+                    for q in range(8):
+                        tl[q, c] = jnp.concatenate([t_in[4 * q + t] for t in range(4)], axis=1)
             else:
                 x_copy.start()
 
@@ -221,6 +245,8 @@
         J = STEPS - k
         base = 4 * k * (k - 1)
         acc[...] = jnp.zeros_like(acc)
+        for rr in range(2):
+            xt[rr, J] = z_in[pl.ds(pl.multiple_of(2048 * rr + 128 * J, 128), 128)].T
 
         def prepare(m, p):
             m = jnp.minimum(m, k - 1)
@@ -304,6 +330,9 @@
 
         @pl.when(k == SWAP)
         def _():
+            for m in range(STEPS - SWAP):
+                xt[ry, m] = z_in[pl.ds(pl.multiple_of(2048 * ry + 128 * m, 128), 128)].T
+
             def stage(m, carry):
                 xs[m] = xt[ry, m]
                 return carry
@@ -314,26 +343,36 @@
 
     lax.fori_loop(1, STEPS + 1, step, 0)
 
-    def half(dst, k, parts, lo, hi):
+    def half(dst, k, parts, lo, hi, put=None):
         def tiles(m, n):
             ds = [mul6(parts, split3(rows(k, 8 * OFF[k], r, m + u)), NN) for u in range(n)]
             for u, d in enumerate(ds):
-                dst[STEPS - k + m + u] = dst[STEPS - k + m + u] - d
+                x = dst[STEPS - k + m + u] - d
+                if put is None:
+                    dst[STEPS - k + m + u] = x
+                else:
+                    here = pl.ds(pl.multiple_of(128 * (m + u), 128), 128)
+                    ob[here, pl.ds(pl.multiple_of(128 * put, 128), 128)] = x.T
 
         by_four(lo, hi, tiles)
 
     last = [yp[i] for i in range(3)]
-    half(xt.at[r], STEPS, last, 0, 4)
+    half(xt.at[r], STEPS, last, 0, 4, r)
     y_copy(REST - 1).start()
-    half(xt.at[r], STEPS, last, 4, STEPS)
-    o_loc = pltpu.make_async_copy(xt.at[r], out_ref.at[r], os.at[2])
-    o_loc.start()
+    half(xt.at[r], STEPS, last, 4, STEPS, r)
     arrive(xn, os.at[1])
     for i in range(REST):
         arrive(yn.at[i], ys.at[1, i])
-        half(xn, SWAP + 1 + i, split3(yn[i]), 0, SWAP + 1 + i)
-    o_nbr = pltpu.make_async_copy(xn, out_ref.at[ry], os.at[3])
-    o_nbr.start()
+        if i < REST - 1:
+            half(xn, SWAP + 1 + i, split3(yn[i]), 0, SWAP + 1 + i)
+    theirs = split3(yn[REST - 1])
+    outs = []
+    for i in range(4):
+        half(xn, STEPS, theirs, 4 * i, 4 * i + 4, ry)
+        here = pl.ds(512 * i, 512)
+        outs.append(pltpu.make_async_copy(ob.at[here], out_ref.at[here], rs.at[LO, 9 + i]))
+        if i:
+            outs[i - 1].start()
 
     for cp in t_copies:
         cp.wait_send()
@@ -344,21 +383,23 @@
     x_copy.wait_send()
     for i in range(REST):
         y_copy(i).wait_send()
-    o_loc.wait()
-    o_nbr.wait()
+    outs[3].start()
+    for cp in outs:
+        cp.wait()
 
 
 def solution(mesh):
     def body(v_loc, t_loc, z_loc):
-        vt = jnp.transpose(v_loc.reshape(16, 128, 1024), (0, 2, 1)).reshape(16, 16, 64, 128)
-        tp = jnp.transpose(t_loc.reshape(8, 4, 32, 32), (0, 2, 1, 3)).reshape(8, 32, 128)
-        zt = jnp.transpose(z_loc.reshape(2, 16, 128, 128), (0, 1, 3, 2))
-        out = pl.pallas_call(
+        return pl.pallas_call(
             kernel,
-            out_shape=jax.ShapeDtypeStruct((2, 16, 128, 128), F32),
+            out_shape=jax.ShapeDtypeStruct((2048, 256), F32),
             in_specs=[pl.BlockSpec(memory_space=pl.ANY)] * 3,
             out_specs=pl.BlockSpec(memory_space=pl.ANY),
             scratch_shapes=[
+                pltpu.VMEM((256 * OFF[9], 128), F32),
+                pltpu.VMEM((32, 32, 32), F32),
+                pltpu.VMEM((4096, 128), F32),
+                pltpu.VMEM((2048, 256), F32),
                 pltpu.VMEM((8 * OFF[STEPS + 1], 64, 128), F32),
                 pltpu.VMEM((8, 4, 32, 128), F32),
                 pltpu.VMEM((2, 16, 128, 128), F32),
@@ -380,8 +421,7 @@
             compiler_params=pltpu.CompilerParams(
                 collective_id=0, has_side_effects=True, vmem_limit_bytes=64 * 1024 * 1024 - 65536
             ),
-        )(vt, tp, zt)
-        return jnp.transpose(out, (1, 3, 0, 2)).reshape(2048, 256)
+        )(v_loc, t_loc, z_loc)
 
     return jax.shard_map(
         body,

time: 211 us -> 192 us (0.910)
  local copies, waits for them, and re-layouts: 18.8 us -> 3.05 us
  Pallas kernels: 192 us -> 189 us
    reshape x5 -> x0, local copies, waits for them, and re-layouts: 17.4 us -> none  [the longest x1 9.26 us: body(): v_loc.reshape(16, 128, 1024)]
    pallas_call x1, Pallas kernels: 192 us -> 189 us  [body(): pl.pallas_call(kernel, out_shape=jax.ShapeDtypeStruct((2048, 256), F32),...]
where the time goes in v6:
time: 192 us
  Pallas kernels  189 us (98%)
  local copies, waits for them, and re-layouts  3.05 us (2%)
    pallas_call x1, Pallas kernels, body(): pl.pallas_call(kernel, out_shape=jax.ShapeDtypeStruct((2048, 256), F32),...  189 us

profile of v6, /device:TPU:0, one launch (start us, length us, event | category | flops | bytes accessed | tf_op | source)
XLA Modules:
  0.0 192.1 jit_solution(14861727361444999605)
XLA Ops:
  0.0 189.0 %shard_map.37 = f32[2048,256]{1,0:T(8,128)} custom-call(f32[2048,1024]{1,0:T(8,128)} %v_ref.1, f32[32,32,32]{2,1,0:T(8,128)} %t_ref.1, f32[4096,128]{1,0:T(8,128)} %z_ref.1), custom_call_target="tpu_custom_call" | custom-call | tf_op jit(solution)/shard_map/pallas_call | solution.py:393
  189.0 3.0 %copy.5 = f32[2048,256]{1,0:T(8,128)} copy(f32[2048,256]{1,0:T(8,128)} %shard_map.37) | data formatting | bytes 4194304

commit v7 on v6

--- a/solution.py
+++ b/solution.py
@@ -264,23 +264,35 @@
         def product(p):
             return mul6([lp[p, i] for i in range(3)], [lp[p, i, 128:384] for i in range(3)], NT)
 
-        def pair(i, carry):
+        def four(i, carry):
             acc[...] += product(0) + product(1)
-            prepare(2 * i + 2, 0)
-            prepare(2 * i + 3, 1)
+            prepare(4 * i + 2, 2)
+            prepare(4 * i + 3, 3)
+            acc[...] += product(2) + product(3)
+            prepare(4 * i + 4, 0)
+            prepare(4 * i + 5, 1)
             return carry
 
-        pairs = lax.div(k, 2)
-        mid = lax.div(pairs + 1, 2)
+        fours, left = lax.div(k, 4), lax.rem(k, 4)
+        mid = lax.div(fours + 1, 2)
         prepare(0, 0)
         prepare(1, 1)
-        lax.fori_loop(0, mid, pair, 0)
+        lax.fori_loop(0, mid, four, 0)
         point(k, MIDDLE)
-        lax.fori_loop(mid, pairs, pair, 0)
-
-        @pl.when(lax.rem(k, 2) == 1)
+        lax.fori_loop(mid, fours, four, 0)
+
+        @pl.when(left == 1)
         def _():
             acc[...] += product(0)
+
+        @pl.when(left >= 2)
+        def _():
+            acc[...] += product(0) + product(1)
+
+        @pl.when(left == 3)
+        def _():
+            prepare(k - 1, 2)
+            acc[...] += product(2)
 
         q, h = J // 2, lax.rem(J, 2)
 
@@ -408,7 +420,7 @@
                 pltpu.VMEM((REST, 128, 256), F32),
                 pltpu.VMEM((REST, 128, 256), F32),
                 pltpu.VMEM((3, 16, 256, 256), BF16),
-                pltpu.VMEM((2, 3, 384, 256), BF16),
+                pltpu.VMEM((4, 3, 384, 256), BF16),
                 pltpu.VMEM((384, 256), F32),
                 pltpu.VMEM((3, 128, 256), BF16),
                 pltpu.SemaphoreType.DMA((10, STEPS + 1)),

time: 192 us -> 190 us (0.990)
  Pallas kernels: 189 us -> 186 us
    pallas_call x1, Pallas kernels: 189 us -> 186 us  [body(): pl.pallas_call(kernel, out_shape=jax.ShapeDtypeStruct((2048, 256), F32),...]
where the time goes in v7:
time: 190 us; the launch traced here: 189 us
  Pallas kernels  186 us (98%)
  local copies, waits for them, and re-layouts  3.05 us (2%)
    pallas_call x1, Pallas kernels, body(): pl.pallas_call(kernel, out_shape=jax.ShapeDtypeStruct((2048, 256), F32),...  186 us

profile of v7, /device:TPU:0, one launch (start us, length us, event | category | flops | bytes accessed | tf_op | source)
XLA Modules:
  0.0 189.0 jit_solution(3290035489483460946)
XLA Ops:
  0.0 185.9 %shard_map.37 = f32[2048,256]{1,0:T(8,128)} custom-call(f32[2048,1024]{1,0:T(8,128)} %v_ref.1, f32[32,32,32]{2,1,0:T(8,128)} %t_ref.1, f32[4096,128]{1,0:T(8,128)} %z_ref.1), custom_call_target="tpu_custom_call" | custom-call | tf_op jit(solution)/shard_map/pallas_call | solution.py:405
  185.9 3.0 %copy.5 = f32[2048,256]{1,0:T(8,128)} copy(f32[2048,256]{1,0:T(8,128)} %shard_map.37) | data formatting | bytes 4194304

commit v8 on v7

--- a/solution.py
+++ b/solution.py
@@ -13,19 +13,18 @@
 OFF = [k * (k - 1) // 2 for k in range(STEPS + 2)]
 NT = (((1,), (1,)), ((), ()))
 NN = (((1,), (0,)), ((), ()))
-SWAP = 13
+SWAP = 14
 REST = STEPS - SWAP
-O, F, D, S, T, X, V = range(7)
+O, F, D, S, T, X, V, E = range(8)
 BEFORE = {k: ((S, k),) for k in range(2, STEPS + 1)}
 BEFORE[1] = ((V, 1), (V, 2), (O, 1), (O, 2), (V, 3), (T, 0), (O, 3), (F, 1), (O, 4), (F, 2), (D, 1), (S, 1))
-BEFORE[14] = ((S, 14), (X, 0))
-BEFORE[15] = ((D, 15), (S, 15))
+BEFORE[14] = ((F, 15), (S, 14))
+BEFORE[15] = ((F, 16), (X, 0), (D, 15), (S, 15))
 MIDDLE = {k: ((F, k + 2), (O, k + 4)) for k in range(1, 13)}
 MIDDLE |= {k: MIDDLE[k] + ((V, (k + 7) // 2),) for k in range(1, 10, 2)}
-MIDDLE[13] = ((F, 15),)
-MIDDLE[14] = ((F, 16),)
+MIDDLE[16] = ((E, 16),)
 AFTER = {k: ((D, k + 1),) for k in (*range(1, 14), 15)}
-ALONG_Y = [0, 0, 1, 1, 2, 2, 3, 3, 4, 4, 5, 5, 6, 6, 7, 7, 0]
+ALONG_Y = [0, 0, 1, 1, 2, 2, 3, 3, 4, 4, 5, 5, 6, 6, 7, 7, 10]
 FX, FY, DX, DY, SO, SX, SY, SD, SE, LO = range(10)
 TX, TY, TS, GX, GY, HX, HY, HD, HE = range(9)
 
@@ -121,7 +120,9 @@
     def c_fwd(k):
         (a0, an), (b0, bn) = halves(k)
         out = []
-        if an:
+        if k == STEPS:
+            out.append(remote(seg(k, ry, c, a0, an), seg(k, ry, c, a0, an), ss.at[GY, k], rs.at[DY, k], to_x))
+        elif an:
             out.append(remote(seg(k, r, cx, a0, an), seg(k, r, cx, a0, an), ss.at[GY, k], rs.at[DY, k], to_y))
         if bn:
             out.append(remote(seg(k, ry, c, b0, bn), seg(k, ry, c, b0, bn), ss.at[GX, k], rs.at[DX, k], to_x))
@@ -153,7 +154,7 @@
         (a0, an), (b0, bn) = halves(k)
         if an:
             arrive(seg(k, ry, cx, a0, an), rs.at[DY, k])
-        if bn:
+        if bn and k < STEPS:
             arrive(seg(k, ry, cx, b0, bn), rs.at[DX, k])
 
     def wait_sib(k):
@@ -163,7 +164,7 @@
         (a0, an), (b0, bn) = halves(k)
         if an:
             arrive(seg(k, ry, csx, a0, an), rs.at[SD, k])
-        if bn:
+        if bn and k < STEPS:
             arrive(seg(k, ry, csx, b0, bn), rs.at[SE, k])
 
     def start_own(k):
@@ -206,8 +207,13 @@
                     t_on.start()
             elif op == D:
                 wait_dia(k)
-                for cp in c_dia(k):
+                for cp in c_dia(k)[: 1 if k == STEPS else 2]:
                     cp.start()
+            elif op == E:
+                b0, bn = halves(k)[1]
+                arrive(seg(k, ry, cx, b0, bn), rs.at[DX, k])
+                c_dia(k)[1].start()
+                arrive(seg(k, ry, csx, b0, bn), rs.at[SE, k])
             elif op == S:
                 wait_sib(k)
                 if k == 1:

time: 190 us -> 188 us (0.989)
  Pallas kernels: 186 us -> 184 us
where the time goes in v8:
time: 188 us; the launch traced here: 187 us
  Pallas kernels  184 us (98%)
  local copies, waits for them, and re-layouts  3.05 us (2%)
    pallas_call x1, Pallas kernels, body(): pl.pallas_call(kernel, out_shape=jax.ShapeDtypeStruct((2048, 256), F32),...  184 us

profile of v8, /device:TPU:0, one launch (start us, length us, event | category | flops | bytes accessed | tf_op | source)
XLA Modules:
  0.0 187.5 jit_solution(7606354024480186857)
XLA Ops:
  0.0 184.4 %shard_map.37 = f32[2048,256]{1,0:T(8,128)} custom-call(f32[2048,1024]{1,0:T(8,128)} %v_ref.1, f32[32,32,32]{2,1,0:T(8,128)} %t_ref.1, f32[4096,128]{1,0:T(8,128)} %z_ref.1), custom_call_target="tpu_custom_call" | custom-call | tf_op jit(solution)/shard_map/pallas_call | solution.py:411
  184.4 3.0 %copy.5 = f32[2048,256]{1,0:T(8,128)} copy(f32[2048,256]{1,0:T(8,128)} %shard_map.37) | data formatting | bytes 4194304

commit v9 on v8

--- a/solution.py
+++ b/solution.py
@@ -15,16 +15,17 @@
 NN = (((1,), (0,)), ((), ()))
 SWAP = 14
 REST = STEPS - SWAP
-O, F, D, S, T, X, V, E = range(8)
+O, F, D, S, T, X, V, E, R, W = range(10)
 BEFORE = {k: ((S, k),) for k in range(2, STEPS + 1)}
-BEFORE[1] = ((V, 1), (V, 2), (O, 1), (O, 2), (V, 3), (T, 0), (O, 3), (F, 1), (O, 4), (F, 2), (D, 1), (S, 1))
+BEFORE[1] = ((V, 1), (V, 2), (O, 1), (O, 2), (V, 3), (T, 0), (O, 3), (O, 4), (F, 1), (F, 2), (D, 1), (S, 1))
 BEFORE[14] = ((F, 15), (S, 14))
-BEFORE[15] = ((F, 16), (X, 0), (D, 15), (S, 15))
+BEFORE[15] = ((F, 16), (X, 0), (W, 13), (D, 15), (S, 15))
+BEFORE[16] = ((S, 16), (E, 16))
 MIDDLE = {k: ((F, k + 2), (O, k + 4)) for k in range(1, 13)}
 MIDDLE |= {k: MIDDLE[k] + ((V, (k + 7) // 2),) for k in range(1, 10, 2)}
-MIDDLE[16] = ((E, 16),)
+MIDDLE[16] = ((R, 16),)
 AFTER = {k: ((D, k + 1),) for k in (*range(1, 14), 15)}
-ALONG_Y = [0, 0, 1, 1, 2, 2, 3, 3, 4, 4, 5, 5, 6, 6, 7, 7, 10]
+ALONG_Y = [0, 0, 1, 1, 2, 2, 3, 4, 4, 5, 5, 6, 6, 7, 7, 5, 10]
 FX, FY, DX, DY, SO, SX, SY, SD, SE, LO = range(10)
 TX, TY, TS, GX, GY, HX, HY, HD, HE = range(9)
 
@@ -193,6 +194,14 @@
 
     def y_copy(i):
         return remote(yo.at[i], yn.at[i], ys.at[0, i], ys.at[1, i], to_y)
+
+    def sent(lo, hi):
+        if lo == 1:
+            for cp in t_copies + [t_on]:
+                cp.wait_send()
+        for k in range(lo, hi + 1):
+            for cp in c_own(k) + c_fwd(k) + c_sib(k) + c_dia(k):
+                cp.wait_send()
 
     def do(ops):
         for op, k in ops:
@@ -213,7 +222,11 @@
                 b0, bn = halves(k)[1]
                 arrive(seg(k, ry, cx, b0, bn), rs.at[DX, k])
                 c_dia(k)[1].start()
+            elif op == R:
+                b0, bn = halves(k)[1]
                 arrive(seg(k, ry, csx, b0, bn), rs.at[SE, k])
+            elif op == W:
+                sent(1, k)
             elif op == S:
                 wait_sib(k)
                 if k == 1:
@@ -392,12 +405,7 @@
         if i:
             outs[i - 1].start()
 
-    for cp in t_copies:
-        cp.wait_send()
-    t_on.wait_send()
-    for k in range(1, STEPS + 1):
-        for cp in c_own(k) + c_fwd(k) + c_sib(k) + c_dia(k):
-            cp.wait_send()
+    sent(14, STEPS)
     x_copy.wait_send()
     for i in range(REST):
         y_copy(i).wait_send()

time: 188 us -> 188 us (level)
  no operation moved by 1% of the time
where the time goes in v9:
time: 188 us
  Pallas kernels  185 us (98%)
  local copies, waits for them, and re-layouts  3.05 us (2%)
    pallas_call x1, Pallas kernels, body(): pl.pallas_call(kernel, out_shape=jax.ShapeDtypeStruct((2048, 256), F32),...  185 us

profile of v9, /device:TPU:0, one launch (start us, length us, event | category | flops | bytes accessed | tf_op | source)
XLA Modules:
  0.0 188.0 jit_solution(3002032746783723661)
XLA Ops:
  0.0 185.0 %shard_map.37 = f32[2048,256]{1,0:T(8,128)} custom-call(f32[2048,1024]{1,0:T(8,128)} %v_ref.1, f32[32,32,32]{2,1,0:T(8,128)} %t_ref.1, f32[4096,128]{1,0:T(8,128)} %z_ref.1), custom_call_target="tpu_custom_call" | custom-call | tf_op jit(solution)/shard_map/pallas_call | solution.py:419
  185.0 3.0 %copy.5 = f32[2048,256]{1,0:T(8,128)} copy(f32[2048,256]{1,0:T(8,128)} %shard_map.37) | data formatting | bytes 4194304

commit v10 on v9

--- a/solution.py
+++ b/solution.py
@@ -19,7 +19,7 @@
 BEFORE = {k: ((S, k),) for k in range(2, STEPS + 1)}
 BEFORE[1] = ((V, 1), (V, 2), (O, 1), (O, 2), (V, 3), (T, 0), (O, 3), (O, 4), (F, 1), (F, 2), (D, 1), (S, 1))
 BEFORE[14] = ((F, 15), (S, 14))
-BEFORE[15] = ((F, 16), (X, 0), (W, 13), (D, 15), (S, 15))
+BEFORE[15] = ((F, 16), (X, 0), (D, 15), (W, 13), (S, 15))
 BEFORE[16] = ((S, 16), (E, 16))
 MIDDLE = {k: ((F, k + 2), (O, k + 4)) for k in range(1, 13)}
 MIDDLE |= {k: MIDDLE[k] + ((V, (k + 7) // 2),) for k in range(1, 10, 2)}

time: 188 us -> 188 us (level)
  no operation moved by 1% of the time
where the time goes in v10:
time: 188 us
  Pallas kernels  185 us (98%)
  local copies, waits for them, and re-layouts  3.05 us (2%)
    pallas_call x1, Pallas kernels, body(): pl.pallas_call(kernel, out_shape=jax.ShapeDtypeStruct((2048, 256), F32),...  185 us

profile of v10, /device:TPU:0, one launch (start us, length us, event | category | flops | bytes accessed | tf_op | source)
XLA Modules:
  0.0 188.0 jit_solution(5619569670909394719)
XLA Ops:
  0.0 185.0 %shard_map.37 = f32[2048,256]{1,0:T(8,128)} custom-call(f32[2048,1024]{1,0:T(8,128)} %v_ref.1, f32[32,32,32]{2,1,0:T(8,128)} %t_ref.1, f32[4096,128]{1,0:T(8,128)} %z_ref.1), custom_call_target="tpu_custom_call" | custom-call | tf_op jit(solution)/shard_map/pallas_call | solution.py:419
  185.0 3.0 %copy.5 = f32[2048,256]{1,0:T(8,128)} copy(f32[2048,256]{1,0:T(8,128)} %shard_map.37) | data formatting | bytes 4194304

commit v11 on v10

--- a/solution.py
+++ b/solution.py
@@ -25,7 +25,7 @@
 MIDDLE |= {k: MIDDLE[k] + ((V, (k + 7) // 2),) for k in range(1, 10, 2)}
 MIDDLE[16] = ((R, 16),)
 AFTER = {k: ((D, k + 1),) for k in (*range(1, 14), 15)}
-ALONG_Y = [0, 0, 1, 1, 2, 2, 3, 4, 4, 5, 5, 6, 6, 7, 7, 5, 10]
+ALONG_Y = [0, 0, 1, 1, 2, 2, 3, 3, 4, 4, 5, 5, 6, 6, 7, 4, 10]
 FX, FY, DX, DY, SO, SX, SY, SD, SE, LO = range(10)
 TX, TY, TS, GX, GY, HX, HY, HD, HE = range(9)
 

time: 188 us -> 190 us (1.011)
  Pallas kernels: 185 us -> 187 us
    pallas_call x1, Pallas kernels: 185 us -> 187 us  [body(): pl.pallas_call(kernel, out_shape=jax.ShapeDtypeStruct((2048, 256), F32),...]
where the time goes in v11:
time: 190 us
  Pallas kernels  187 us (98%)
  local copies, waits for them, and re-layouts  3.05 us (2%)
    pallas_call x1, Pallas kernels, body(): pl.pallas_call(kernel, out_shape=jax.ShapeDtypeStruct((2048, 256), F32),...  187 us

profile of v11, /device:TPU:0, one launch (start us, length us, event | category | flops | bytes accessed | tf_op | source)
XLA Modules:
  0.0 190.3 jit_solution(10075038722119235636)
XLA Ops:
  0.0 187.2 %shard_map.37 = f32[2048,256]{1,0:T(8,128)} custom-call(f32[2048,1024]{1,0:T(8,128)} %v_ref.1, f32[32,32,32]{2,1,0:T(8,128)} %t_ref.1, f32[4096,128]{1,0:T(8,128)} %z_ref.1), custom_call_target="tpu_custom_call" | custom-call | tf_op jit(solution)/shard_map/pallas_call | solution.py:419
  187.2 3.0 %copy.5 = f32[2048,256]{1,0:T(8,128)} copy(f32[2048,256]{1,0:T(8,128)} %shard_map.37) | data formatting | bytes 4194304

commit v12 on v11

--- a/solution.py
+++ b/solution.py
@@ -25,7 +25,7 @@
 MIDDLE |= {k: MIDDLE[k] + ((V, (k + 7) // 2),) for k in range(1, 10, 2)}
 MIDDLE[16] = ((R, 16),)
 AFTER = {k: ((D, k + 1),) for k in (*range(1, 14), 15)}
-ALONG_Y = [0, 0, 1, 1, 2, 2, 3, 3, 4, 4, 5, 5, 6, 6, 7, 4, 10]
+ALONG_Y = [0, 0, 1, 1, 2, 2, 3, 3, 4, 5, 5, 6, 6, 7, 7, 7, 10]
 FX, FY, DX, DY, SO, SX, SY, SD, SE, LO = range(10)
 TX, TY, TS, GX, GY, HX, HY, HD, HE = range(9)
 

time: 190 us -> 189 us (level)
  no operation moved by 1% of the time
where the time goes in v12:
time: 189 us
  Pallas kernels  186 us (98%)
  local copies, waits for them, and re-layouts  3.05 us (2%)
    pallas_call x1, Pallas kernels, body(): pl.pallas_call(kernel, out_shape=jax.ShapeDtypeStruct((2048, 256), F32),...  186 us

profile of v12, /device:TPU:0, one launch (start us, length us, event | category | flops | bytes accessed | tf_op | source)
XLA Modules:
  0.0 189.0 jit_solution(3857211027229180215)
XLA Ops:
  0.0 185.9 %shard_map.37 = f32[2048,256]{1,0:T(8,128)} custom-call(f32[2048,1024]{1,0:T(8,128)} %v_ref.1, f32[32,32,32]{2,1,0:T(8,128)} %t_ref.1, f32[4096,128]{1,0:T(8,128)} %z_ref.1), custom_call_target="tpu_custom_call" | custom-call | tf_op jit(solution)/shard_map/pallas_call | solution.py:419
  185.9 3.0 %copy.5 = f32[2048,256]{1,0:T(8,128)} copy(f32[2048,256]{1,0:T(8,128)} %shard_map.37) | data formatting | bytes 4194304

commit v13 on v12

--- a/solution.py
+++ b/solution.py
@@ -20,12 +20,12 @@
 BEFORE[1] = ((V, 1), (V, 2), (O, 1), (O, 2), (V, 3), (T, 0), (O, 3), (O, 4), (F, 1), (F, 2), (D, 1), (S, 1))
 BEFORE[14] = ((F, 15), (S, 14))
 BEFORE[15] = ((F, 16), (X, 0), (D, 15), (W, 13), (S, 15))
-BEFORE[16] = ((S, 16), (E, 16))
+BEFORE[16] = ((S, 16),)
 MIDDLE = {k: ((F, k + 2), (O, k + 4)) for k in range(1, 13)}
 MIDDLE |= {k: MIDDLE[k] + ((V, (k + 7) // 2),) for k in range(1, 10, 2)}
-MIDDLE[16] = ((R, 16),)
+MIDDLE[16] = ((E, 16), (R, 16))
 AFTER = {k: ((D, k + 1),) for k in (*range(1, 14), 15)}
-ALONG_Y = [0, 0, 1, 1, 2, 2, 3, 3, 4, 5, 5, 6, 6, 7, 7, 7, 10]
+ALONG_Y = [0, 0, 1, 1, 2, 2, 3, 3, 4, 4, 5, 5, 6, 6, 7, 7, 10]
 FX, FY, DX, DY, SO, SX, SY, SD, SE, LO = range(10)
 TX, TY, TS, GX, GY, HX, HY, HD, HE = range(9)
 

time: 189 us -> 190 us (level)
  no operation moved by 1% of the time
where the time goes in v13:
time: 190 us
  Pallas kernels  187 us (98%)
  local copies, waits for them, and re-layouts  3.05 us (2%)
    pallas_call x1, Pallas kernels, body(): pl.pallas_call(kernel, out_shape=jax.ShapeDtypeStruct((2048, 256), F32),...  187 us

profile of v13, /device:TPU:0, one launch (start us, length us, event | category | flops | bytes accessed | tf_op | source)
XLA Modules:
  0.0 189.7 jit_solution(7056918182559414727)
XLA Ops:
  0.0 186.7 %shard_map.37 = f32[2048,256]{1,0:T(8,128)} custom-call(f32[2048,1024]{1,0:T(8,128)} %v_ref.1, f32[32,32,32]{2,1,0:T(8,128)} %t_ref.1, f32[4096,128]{1,0:T(8,128)} %z_ref.1), custom_call_target="tpu_custom_call" | custom-call | tf_op jit(solution)/shard_map/pallas_call | solution.py:419
  186.7 3.0 %copy.5 = f32[2048,256]{1,0:T(8,128)} copy(f32[2048,256]{1,0:T(8,128)} %shard_map.37) | data formatting | bytes 4194304

commit v14 on v10

--- a/solution.py
+++ b/solution.py
@@ -17,7 +17,7 @@
 REST = STEPS - SWAP
 O, F, D, S, T, X, V, E, R, W = range(10)
 BEFORE = {k: ((S, k),) for k in range(2, STEPS + 1)}
-BEFORE[1] = ((V, 1), (V, 2), (O, 1), (O, 2), (V, 3), (T, 0), (O, 3), (O, 4), (F, 1), (F, 2), (D, 1), (S, 1))
+BEFORE[1] = ((V, 1), (V, 2), (O, 1), (O, 2), (V, 3), (T, 0), (O, 3), (F, 1), (O, 4), (F, 2), (D, 1), (S, 1))
 BEFORE[14] = ((F, 15), (S, 14))
 BEFORE[15] = ((F, 16), (X, 0), (D, 15), (W, 13), (S, 15))
 BEFORE[16] = ((S, 16), (E, 16))

time: 188 us -> 186 us (0.989)
  Pallas kernels: 185 us -> 183 us
    pallas_call x1, Pallas kernels: 185 us -> 183 us  [body(): pl.pallas_call(kernel, out_shape=jax.ShapeDtypeStruct((2048, 256), F32),...]
where the time goes in v14:
time: 186 us
  Pallas kernels  183 us (98%)
  local copies, waits for them, and re-layouts  3.05 us (2%)
    pallas_call x1, Pallas kernels, body(): pl.pallas_call(kernel, out_shape=jax.ShapeDtypeStruct((2048, 256), F32),...  183 us

profile of v14, /device:TPU:0, one launch (start us, length us, event | category | flops | bytes accessed | tf_op | source)
XLA Modules:
  0.0 185.7 jit_solution(11700600660497773858)
XLA Ops:
  0.0 182.7 %shard_map.37 = f32[2048,256]{1,0:T(8,128)} custom-call(f32[2048,1024]{1,0:T(8,128)} %v_ref.1, f32[32,32,32]{2,1,0:T(8,128)} %t_ref.1, f32[4096,128]{1,0:T(8,128)} %z_ref.1), custom_call_target="tpu_custom_call" | custom-call | tf_op jit(solution)/shard_map/pallas_call | solution.py:419
  182.7 3.0 %copy.5 = f32[2048,256]{1,0:T(8,128)} copy(f32[2048,256]{1,0:T(8,128)} %shard_map.37) | data formatting | bytes 4194304
